TPU v7x, 32 devices: a whole 2x2x4 slice. The times are simulated.
32 devices in a mesh: dp: 4 (over y, x), frame: 2 (over core), tensor: 4 (over z).
Axes of the slice: x: 2, y: 2, z: 4, core: 2. Of those that a mesh axis runs over, the one named last changes fastest.
Arguments:
- tokens: bfloat16 [8, 8, 256, 1024], P('dp', ('frame', 'tensor')), may hold values from -6 to 6
- out_grad: bfloat16 [8, 8, 256, 1024], P('dp', ('frame', 'tensor')), may hold values from -6 to 6
- noise_index: int32 [8, 8], P('dp', 'frame'), may hold values from 0 to 999, as said below
- qkv_weight: bfloat16 [1024, 3, 1024], P(('dp', 'frame'), None, 'tensor'), may hold values from -0.1875 to 0.1875
- out_weight: bfloat16 [1024, 1024], P(('dp', 'frame'), 'tensor'), may hold values from -0.75 to 0.75
- up_weight: bfloat16 [1024, 4096], P(('dp', 'frame'), 'tensor'), may hold values from -0.1875 to 0.1875
- down_weight: bfloat16 [1024, 4096], P(('dp', 'frame'), 'tensor'), may hold values from -0.09375 to 0.09375
- ada_weight: bfloat16 [1024, 6, 1024], P(('dp', 'frame'), None, 'tensor'), may hold values from -0.25 to 0.25
Outputs:
- result: bfloat16 [8, 8, 256, 1024], P('dp', ('frame', 'tensor'))
- input_grad: bfloat16 [8, 8, 256, 1024], P('dp', ('frame', 'tensor'))
- qkv_grad: float32 [1024, 3, 1024], P(('dp', 'frame'), None, 'tensor')
- out_weight_grad: float32 [1024, 1024], P(('dp', 'frame'), 'tensor')
- up_grad: float32 [1024, 4096], P(('dp', 'frame'), 'tensor')
- down_grad: float32 [1024, 4096], P(('dp', 'frame'), 'tensor')
- ada_grad: float32 [1024, 6, 1024], P(('dp', 'frame'), None, 'tensor')
Inputs may be any that keep to these rules, and one draw needn't show every extreme that they name: `noise_index`: each frame's noise level, most often near 1000 - 1.
All inputs are finite; a program needn't handle non-finite values.
Results may differ from a plain program's by a relative error of at most 0.018.
Values may be sent and summed in bfloat16 or wider, within the bound.
A program may use at most 192 MiB of HBM per device.

v0:
```python
import math
import jax
import jax.numpy as jnp
from jax import lax
from jax.sharding import PartitionSpec as P

HEAD_DIM = 64
epsilon = 1e-06
highest = lax.Precision.HIGHEST


def normalize(values):
    center = values - jnp.mean(values, axis=-1, keepdims=True)
    spread = jnp.mean(center * center, axis=-1, keepdims=True)
    inverse = lax.rsqrt(spread + epsilon)
    return (center * inverse, inverse)


def norm_back(upstream, normed, inverse):
    upstream_mean = jnp.mean(upstream, axis=-1, keepdims=True)
    product_mean = jnp.mean(upstream * normed, axis=-1, keepdims=True)
    return inverse * (upstream - upstream_mean - normed * product_mean)


def level_embedding(levels, model_width):
    halfway = model_width // 2
    frequency = jnp.exp(-math.log(10000.0) * jnp.arange(halfway, dtype=jnp.float32) / halfway)
    angles = levels.astype(jnp.float32)[..., None] * frequency
    return jnp.concatenate([jnp.cos(angles), jnp.sin(angles)], axis=-1)


def gelu_tanh(values):
    return jax.nn.gelu(values, approximate=True)


def on_device(
    tokens, out_grad, noise_index, qkv_weight, out_weight, up_weight, down_weight, ada_weight
):
    clips = tokens.shape[0]
    patches = tokens.shape[2]
    model_width = tokens.shape[-1]
    local_width = qkv_weight.shape[2]
    rows_here = qkv_weight.shape[0]
    heads_here = local_width // HEAD_DIM
    scaling = HEAD_DIM ** (-0.5)
    groups = lax.axis_size("tensor")
    halves = lax.axis_size("frame")
    replicas = lax.axis_size("dp")
    with jax.named_scope("modulation"):
        levels_all = lax.all_gather(noise_index, ("dp", "frame"), axis=0, tiled=True)
        levels_all = levels_all.reshape(replicas * halves, clips, groups)
        condition_all = jax.nn.silu(level_embedding(levels_all, model_width)).astype(jnp.bfloat16)
        row_block = lax.axis_index("dp") * halves + lax.axis_index("frame")
        my_condition = lax.dynamic_slice_in_dim(
            condition_all, row_block * rows_here, rows_here, axis=3
        )
        partial_mod = jnp.einsum(
            "acgd,dkw->acgkw", my_condition, ada_weight, preferred_element_type=jnp.float32
        )
        summed_mod = jnp.sum(lax.all_to_all(partial_mod, ("dp", "frame"), 0, 0, tiled=True), axis=0)
        group_mod = lax.all_gather(summed_mod, "tensor", axis=3, tiled=True)
        group_mod = jnp.swapaxes(group_mod, 1, 2)[:, :, :, None, :]
        group_index = lax.axis_index("tensor")
        modulation = lax.dynamic_index_in_dim(group_mod, group_index, axis=2, keepdims=False)
    with jax.named_scope("weights"):
        joint_weight, mixer_weight, upward_weight, downward_weight = (
            lax.all_gather(w, ("dp", "frame"), axis=0, tiled=True)
            for w in (qkv_weight, out_weight, up_weight, down_weight)
        )
    residual = tokens[:, 0].astype(jnp.float32)
    upstream = out_grad[:, 0].astype(jnp.float32)
    with jax.named_scope("group_inputs"):
        group_tokens = lax.all_gather(tokens[:, 0], "tensor", axis=1, tiled=True)
        group_upstream = lax.all_gather(out_grad[:, 0], "tensor", axis=1, tiled=True)

    def gather_halves(values):
        if halves != 2:
            return lax.all_gather(values, "frame", axis=1, tiled=True)
        other = lax.ppermute(values, "frame", [(0, 1), (1, 0)])
        return jnp.concatenate([values, other], axis=1)

    def scatter_halves(values):
        if halves != 2:
            return lax.psum_scatter(
                values.astype(jnp.bfloat16), "frame", scatter_dimension=1, tiled=True
            ).astype(jnp.float32)
        count = values.shape[1] // 2
        mine = values[:, :count]
        other = lax.ppermute(values[:, count:].astype(jnp.bfloat16), "frame", [(0, 1), (1, 0)])
        return mine.astype(jnp.bfloat16).astype(jnp.float32) + other.astype(jnp.float32)

    def clip_pass(residual, upstream, modulation, group_tokens, group_upstream, group_mod):
        clips = residual.shape[0]
        patches = residual.shape[1]
        shift1, scale1, gate1 = (modulation[:, 0], modulation[:, 1], modulation[:, 2])
        shift2, scale2, gate2 = (modulation[:, 3], modulation[:, 4], modulation[:, 5])

        def gather_tokens(values):
            return lax.all_gather(values, "tensor", axis=1, tiled=True)

        def scatter_tokens(values):
            parts = values.astype(jnp.bfloat16).reshape(
                values.shape[0], groups, -1, values.shape[-1]
            )
            received = lax.all_to_all(parts, "tensor", 1, 1, tiled=True)
            return jnp.sum(received.astype(jnp.float32), axis=1)

        with jax.named_scope("forward"):
            normed_one, inverse_one = normalize(residual)
            group_normed, _ = normalize(
                group_tokens.astype(jnp.float32).reshape(clips, groups, patches, model_width)
            )
            flat_one = (
                (group_normed * (1.0 + group_mod[:, 1]) + group_mod[:, 0])
                .astype(jnp.bfloat16)
                .reshape(clips, groups * patches, model_width)
            )
            token_count = flat_one.shape[1]
            projected = jnp.einsum(
                "crd,dkh->crkh", flat_one, joint_weight, preferred_element_type=jnp.float32
            ).astype(jnp.bfloat16)
            queries = projected[:, :, 0]
            keys_all = gather_halves(projected[:, :, 1])
            values_all = gather_halves(projected[:, :, 2])
            key_heads = keys_all.reshape(clips, -1, heads_here, HEAD_DIM)
            value_heads = values_all.reshape(clips, -1, heads_here, HEAD_DIM)
            block_rows = min(512, token_count)
            block_count = token_count // block_rows
            query_blocks = jnp.moveaxis(
                queries.reshape(clips, block_count, block_rows, heads_here, HEAD_DIM), 1, 0
            )

            def attend(query_block):
                scores = (
                    jnp.einsum(
                        "cqhe,ckhe->chqk",
                        query_block,
                        key_heads,
                        preferred_element_type=jnp.float32,
                    )
                    * scaling
                )
                largest = jnp.max(scores, axis=-1, keepdims=True)
                raised = jnp.exp(scores - largest)
                totals_row = jnp.sum(raised, axis=-1, keepdims=True)
                probs_low = (raised / totals_row).astype(jnp.bfloat16)
                outputs = jnp.einsum(
                    "chqk,ckhe->cqhe", probs_low, value_heads, preferred_element_type=jnp.float32
                )
                return (outputs.astype(jnp.bfloat16), (largest + jnp.log(totals_row))[..., 0])

            attended_blocks, log_totals = lax.map(attend, query_blocks)
            attended = jnp.moveaxis(attended_blocks, 0, 1).reshape(clips, token_count, local_width)
            partial_one = jnp.einsum(
                "crh,oh->cro", attended, mixer_weight, preferred_element_type=jnp.float32
            )
            branch_one = scatter_tokens(partial_one)
            middle = residual + gate1 * branch_one
            normed_two, inverse_two = normalize(middle)
            entering_two = (normed_two * (1.0 + scale2) + shift2).astype(jnp.bfloat16)
            flat_two = gather_tokens(entering_two)
            up_values = jnp.einsum(
                "crd,df->crf", flat_two, upward_weight, preferred_element_type=jnp.float32
            )
            hidden = gelu_tanh(up_values).astype(jnp.bfloat16)
            partial_two = jnp.einsum(
                "crf,of->cro", hidden, downward_weight, preferred_element_type=jnp.float32
            )
            branch_two = scatter_tokens(partial_two)
            output = (middle + gate2 * branch_two).astype(jnp.bfloat16)
        with jax.named_scope("backward_ffn"):
            grad_gate_two = jnp.sum(upstream * branch_two, axis=1)
            grad_two_all = (
                (
                    group_mod[:, 5]
                    * group_upstream.astype(jnp.float32).reshape(
                        clips, groups, patches, model_width
                    )
                )
                .astype(jnp.bfloat16)
                .reshape(clips, groups * patches, model_width)
            )
            grad_hidden = jnp.einsum(
                "cro,of->crf", grad_two_all, downward_weight, preferred_element_type=jnp.float32
            )
            down_total = jnp.einsum(
                "cro,crf->of", grad_two_all, hidden, preferred_element_type=jnp.float32
            )
            _, gelu_pullback = jax.vjp(gelu_tanh, up_values)
            grad_up = gelu_pullback(grad_hidden)[0].astype(jnp.bfloat16)
            up_total = jnp.einsum(
                "crd,crf->df", flat_two, grad_up, preferred_element_type=jnp.float32
            )
            partial_back_two = jnp.einsum(
                "crf,df->crd", grad_up, upward_weight, preferred_element_type=jnp.float32
            )
            grad_entering_two = scatter_tokens(partial_back_two)
            grad_shift_two = jnp.sum(grad_entering_two, axis=1)
            grad_scale_two = jnp.sum(grad_entering_two * normed_two, axis=1)
            grad_middle = upstream + norm_back(
                grad_entering_two * (1.0 + scale2), normed_two, inverse_two
            )
            grad_gate_one = jnp.sum(grad_middle * branch_one, axis=1)
        with jax.named_scope("backward_attention"):
            grad_branch_one = (gate1 * grad_middle).astype(jnp.bfloat16)
            grad_one_all = gather_tokens(grad_branch_one)
            grad_attended = jnp.einsum(
                "cro,oh->crh", grad_one_all, mixer_weight, preferred_element_type=jnp.float32
            ).astype(jnp.bfloat16)
            mixer_total = jnp.einsum(
                "cro,crh->oh", grad_one_all, attended, preferred_element_type=jnp.float32
            )
            grad_blocks = jnp.moveaxis(
                grad_attended.reshape(clips, block_count, block_rows, heads_here, HEAD_DIM), 1, 0
            )

            def attend_back(carried, pieces):
                key_sum, value_sum = carried
                query_block, grad_block, log_block = pieces
                scores = (
                    jnp.einsum(
                        "cqhe,ckhe->chqk",
                        query_block,
                        key_heads,
                        preferred_element_type=jnp.float32,
                    )
                    * scaling
                )
                probs = jnp.exp(scores - log_block[..., None])
                grad_probs = jnp.einsum(
                    "cqhe,ckhe->chqk", grad_block, value_heads, preferred_element_type=jnp.float32
                )
                value_sum = value_sum + jnp.einsum(
                    "chqk,cqhe->ckhe",
                    probs.astype(jnp.bfloat16),
                    grad_block,
                    preferred_element_type=jnp.float32,
                )
                row_terms = jnp.sum(probs * grad_probs, axis=-1, keepdims=True)
                grad_scores = (probs * (grad_probs - row_terms)).astype(jnp.bfloat16)
                grad_queries = (
                    jnp.einsum(
                        "chqk,ckhe->cqhe",
                        grad_scores,
                        key_heads,
                        preferred_element_type=jnp.float32,
                    )
                    * scaling
                )
                key_sum = (
                    key_sum
                    + jnp.einsum(
                        "chqk,cqhe->ckhe",
                        grad_scores,
                        query_block,
                        preferred_element_type=jnp.float32,
                    )
                    * scaling
                )
                return ((key_sum, value_sum), grad_queries)

            zeros_keys = jnp.zeros(key_heads.shape, jnp.float32)
            (key_grads, value_grads), query_grads = lax.scan(
                attend_back, (zeros_keys, zeros_keys), (query_blocks, grad_blocks, log_totals)
            )
            query_grads = jnp.moveaxis(query_grads, 0, 1).reshape(clips, token_count, local_width)
            key_own, value_own = (
                scatter_halves(grads.reshape(clips, -1, local_width))
                for grads in (key_grads, value_grads)
            )
            grad_projected = jnp.stack([query_grads, key_own, value_own], axis=2).astype(
                jnp.bfloat16
            )
            joint_total = jnp.einsum(
                "crd,crkh->dkh", flat_one, grad_projected, preferred_element_type=jnp.float32
            )
            partial_back_one = jnp.einsum(
                "crkh,dkh->crd", grad_projected, joint_weight, preferred_element_type=jnp.float32
            )
            grad_entering_one = scatter_tokens(partial_back_one)
            grad_shift_one = jnp.sum(grad_entering_one, axis=1)
            grad_scale_one = jnp.sum(grad_entering_one * normed_one, axis=1)
            grad_input = grad_middle + norm_back(
                grad_entering_one * (1.0 + scale1), normed_one, inverse_one
            )
        grad_modulation = jnp.stack(
            [
                grad_shift_one,
                grad_scale_one,
                grad_gate_one,
                grad_shift_two,
                grad_scale_two,
                grad_gate_two,
            ],
            axis=1,
        )
        totals = (joint_total, mixer_total, up_total, down_total)
        return (output, grad_input.astype(jnp.bfloat16), grad_modulation, totals)

    pieces = [
        clip_pass(
            residual[i : i + 1],
            upstream[i : i + 1],
            modulation[i : i + 1],
            group_tokens[i : i + 1],
            group_upstream[i : i + 1],
            group_mod[i : i + 1],
        )
        for i in range(clips)
    ]
    output = jnp.concatenate([p[0] for p in pieces], axis=0)
    grad_input_low = jnp.concatenate([p[1] for p in pieces], axis=0)
    grad_modulation = jnp.concatenate([p[2] for p in pieces], axis=0)
    joint_total, mixer_total, up_total, down_total = (
        sum((p[3][k] for p in pieces[1:])) + pieces[0][3][k] for k in range(4)
    )
    with jax.named_scope("ada_grad"):
        grad_columns = lax.all_to_all(
            grad_modulation.reshape(clips, 1, 6, model_width), "tensor", 3, 1, tiled=True
        )
        grad_all = lax.all_gather(grad_columns, ("dp", "frame"), axis=0, tiled=True)
        grad_all = grad_all.reshape(replicas * halves, clips, groups, 6, local_width)
        adaptive_total = jnp.einsum(
            "acgd,acgkw->dkw", my_condition.astype(jnp.float32), grad_all, precision=highest
        )
    with jax.named_scope("weight_grads"):
        summed = tuple(
            (
                lax.psum_scatter(
                    total.astype(jnp.bfloat16), ("dp", "frame"), scatter_dimension=0, tiled=True
                ).astype(jnp.float32)
                for total in (joint_total, mixer_total, up_total, down_total)
            )
        )
    result = output[:, None]
    input_grad = grad_input_low[:, None]
    return (result, input_grad, summed[0], summed[1], summed[2], summed[3], adaptive_total)


def solution(mesh):
    return jax.shard_map(
        on_device,
        mesh=mesh,
        in_specs=(
            P("dp", ("frame", "tensor"), None, None),
            P("dp", ("frame", "tensor"), None, None),
            P("dp", "frame"),
            P(("dp", "frame"), None, "tensor"),
            P(("dp", "frame"), "tensor"),
            P(("dp", "frame"), "tensor"),
            P(("dp", "frame"), "tensor"),
            P(("dp", "frame"), None, "tensor"),
        ),
        out_specs=(
            P("dp", ("frame", "tensor"), None, None),
            P("dp", ("frame", "tensor"), None, None),
            P(("dp", "frame"), None, "tensor"),
            P(("dp", "frame"), "tensor"),
            P(("dp", "frame"), "tensor"),
            P(("dp", "frame"), "tensor"),
            P(("dp", "frame"), None, "tensor"),
        ),
        check_vma=False,
    )
```

profile of v0, /device:TPU:0, one launch (start us, length us, event | category | flops | bytes accessed | tf_op | source)
XLA Modules:
  0.0 1021.4 jit_solution(15384394116283009315)
XLA Ops:
  10.5 10.6 %all-gather.3 = s32[8,2,4]{2,1,0:T(2,128)S(1)} all-gather(s32[1,2,4]{2,1,0:T(2,128)} %bitcast.739), channel_id=1, replica_groups=mesh['dp'=4,'frame'=2,'tensor'=4] {'dp','frame'}, dimensions={0}, use_global_device_ids=true | all-gather | bytes 288 | tf_op jit(solution)/shard_map/modulation/all_gather | solution.py:50
  27.3 12.8 %all_gather.43 = bf16[1024,256]{1,0:T(8,128)(2,1)} all-gather(bf16[128,256]{1,0:T(8,128)(2,1)S(1)} %copy-done.71), channel_id=1, replica_groups=mesh['dp'=4,'frame'=2,'tensor'=4] {'dp','frame'}, dimensions={0}, use_global_device_ids=true | all-gather | bytes 589824 | tf_op jit(solution)/shard_map/weights/all_gather | solution.py:67
  40.3 19.4 %all_gather.40 = f32[2,4,6,1024]{3,2,1,0:T(8,128)S(1)} all-gather(f32[2,4,6,256]{3,2,1,0:T(8,128)S(1)} %copy.337), channel_id=1, replica_groups=mesh['dp'=4,'frame'=2,'tensor'=4] {'tensor'}, dimensions={3}, use_global_device_ids=true | all-gather | bytes 245760 | tf_op jit(solution)/shard_map/modulation/all_gather | solution.py:61
  61.0 36.2 %all-gather.28.cloned.1.call-done = bf16[2,1,1024,1024]{3,2,1,0:T(8,128)(2,1)} async-done(((bf16[2,1,256,1024]{3,2,1,0:T(8,128)(2,1)}), bf16[2,1,1024,1024]{3,2,1,0:T(8,128)(2,1)}) %all-gather.28.cloned.1.call-update) | async-done | bytes 4194320 | tf_op jit(solution)/shard_map/group_inputs/all_gather | solution.py:73
  107.8 16.2 %all-gather.14.cloned.1.call-done = bf16[1024,3,256]{0,2,1:T(8,128)(2,1)} async-done(((bf16[128,3,256]{0,2,1:T(8,128)(2,1)}), bf16[1024,3,256]{0,2,1:T(8,128)(2,1)}) %all-gather.14.cloned.1.call-update) | async-done | bytes 1572880 | tf_op jit(solution)/shard_map/weights/all_gather | solution.py:67
  140.7 21.9 %while.55 = (s32[]{:T(128)}, bf16[2,1,512,4,64]{2,4,3,1,0:T(8,128)(2,1)}, f32[2,1,4,512]{3,2,1,0:T(4,128)S(1)}, bf16[2,1,512,4,64]{2,4,3,1,0:T(8,128)(2,1)S(1)},...) while((s32[]{:T(128)}, ...), condition=%wide.region_16.17_spmd, body=%wide.region_13.16_spmd.sunk | while | flops 1111619584 | bytes 53019220 | solution.py:152
  157.3 5.1 fusion.283
  174.9 21.8 %while.54 = (s32[]{:T(128)}, bf16[2,1,512,4,64]{2,4,3,1,0:T(8,128)(2,1)}, f32[2,1,4,512]{3,2,1,0:T(4,128)S(1)}, bf16[2,1,512,4,64]{2,4,3,1,0:T(8,128)(2,1)S(1)},...) while((s32[]{:T(128)}, bf16[2,1,512,4,64]{2,4,3,1,0:T(8,128)(2,1)}, ...), condition=%wide.region_6.7_spmd, body=%wide.region_3.0_spmd.sunk | while | flops 1111619584 | bytes 53019220 | solution.py:152
  201.6 49.2 %all-to-all-done.3 = bf16[1,4,256,1024]{3,2,0,1:T(8,128)(2,1)} async-done(((bf16[1,4,256,1024]{3,2,0,1:T(8,128)(2,1)}), bf16[1,4,256,1024]{3,2,0,1:T(8,128)(2,1)}, u32[]{:S(2)}, u32[]{:S(2)}) %all-to-all-start.3) | async-done | bytes 2097184 | tf_op jit(solution)/shard_map/forward/all_to_all | solution.py:105
  261.7 42.4 %all-to-all-done.1 = bf16[1,4,256,1024]{3,2,0,1:T(8,128)(2,1)} async-done(((bf16[1,4,256,1024]{3,2,0,1:T(8,128)(2,1)}), bf16[1,4,256,1024]{3,2,0,1:T(8,128)(2,1)}, u32[]{:S(2)}, u32[]{:S(2)}) %all-to-all-start.1) | async-done | bytes 2097184 | tf_op jit(solution)/shard_map/forward/all_to_all | solution.py:105
  312.2 5.6 fusion.107
  317.8 6.9 fusion.211
  326.0 30.3 %all-gather.22.cloned.1.call-done = bf16[1,1024,1024]{2,1,0:T(8,128)(2,1)} async-done(((bf16[1,256,1024]{2,1,0:T(8,128)(2,1)}), bf16[1,1024,1024]{2,1,0:T(8,128)(2,1)}) %all-gather.22.cloned.1.call-update) | async-done | bytes 2097168 | tf_op jit(solution)/shard_map/forward/all_gather | solution.py:99
  356.3 10.1 fusion.125
  374.9 6.6 fusion.210
  381.6 56.0 %all-gather.16.cloned.1.call-done = bf16[1,1024,1024]{2,1,0:T(8,128)(2,1)} async-done(((bf16[1,256,1024]{2,1,0:T(8,128)(2,1)}), bf16[1,1024,1024]{2,1,0:T(8,128)(2,1)}) %all-gather.16.cloned.1.call-update) | async-done | bytes 2097168 | tf_op jit(solution)/shard_map/forward/all_gather | solution.py:99
  437.6 10.1 fusion.118
  457.2 6.9 convolution_convert_fusion.2
  464.2 39.3 %all-to-all-done.5 = bf16[1,4,256,1024]{3,2,0,1:T(8,128)(2,1)} async-done(((bf16[1,4,256,1024]{3,2,0,1:T(8,128)(2,1)}), bf16[1,4,256,1024]{3,2,0,1:T(8,128)(2,1)}, u32[]{:S(2)}, u32[]{:S(2)}) %all-to-all-start.5) | async-done | bytes 2097184 | tf_op jit(solution)/shard_map/backward_ffn/all_to_all | solution.py:105
  509.6 6.9 convolution_convert_fusion.4
  516.5 39.3 %all-to-all-done.4 = bf16[1,4,256,1024]{3,2,0,1:T(8,128)(2,1)} async-done(((bf16[1,4,256,1024]{3,2,0,1:T(8,128)(2,1)}), bf16[1,4,256,1024]{3,2,0,1:T(8,128)(2,1)}, u32[]{:S(2)}, u32[]{:S(2)}) %all-to-all-start.4) | async-done | bytes 2097184 | tf_op jit(solution)/shard_map/forward/all_to_all | solution.py:105
  574.4 67.3 %all-to-all-done.2 = bf16[1,4,256,1024]{3,2,0,1:T(8,128)(2,1)} async-done(((bf16[1,4,256,1024]{3,2,0,1:T(8,128)(2,1)}), bf16[1,4,256,1024]{3,2,0,1:T(8,128)(2,1)}, u32[]{:S(2)}, u32[]{:S(2)}) %all-to-all-start.2) | async-done | bytes 2097184 | tf_op jit(solution)/shard_map/forward/all_to_all | solution.py:105
  653.4 5.2 fusion.197
  680.0 87.2 %while.57 = (s32[]{:T(128)}, f32[1,2048,4,64]{1,3,2,0:T(8,128)}, f32[1,2048,4,64]{1,3,2,0:T(8,128)}, bf16[2,1,512,4,64]{2,4,3,1,0:T(8,128)(2,1)}, bf16[2,1,512,4...) while((s32[]{:T(128)}, f32[1,2048,4,64]{1,3,2,0:T(8,128)}, ...), condition=%wide.region_39.40_spmd.clone, body=%wide.region_37.39_spmd.clone.sunk | while | flops 2737436672 | bytes 273212096 | solution.py:263
  682.5 8.6 multiply_reduce_fusion.23
  693.3 10.6 %multiply_convert_fusion.14 = bf16[4,512,2048]{2,1,0:T(8,128)(2,1)} fusion(f32[4,512,2048]{2,1,0:T(8,128)} %get-tuple-element.848, f32[4,512,2048]{2,1,0:T(8,128)S(1)} %fusion.304, f32[4,512]{1,0:T(4,128)S(1)} %get-tuple-element.849, f32[4,512]{1,0:T(4,128)S(1)} %dynamic-slice_bitcast_fusion.7), kind=kLoop, calls=%fused_computation.66.clone.1 | loop fusion | flops 20971520 | bytes 41959424 | tf_op jit(solution)/shard_map/backward_attention/while/body/eval_jaxpr/convert_element_type | solution.py:240
  703.9 6.9 fusion.305
  710.8 7.5 fusion.307
  725.1 8.6 multiply_reduce_fusion.23
  736.0 10.4 %multiply_convert_fusion.14 = bf16[4,512,2048]{2,1,0:T(8,128)(2,1)} fusion(f32[4,512,2048]{2,1,0:T(8,128)} %get-tuple-element.848, f32[4,512,2048]{2,1,0:T(8,128)S(1)} %fusion.304, f32[4,512]{1,0:T(4,128)S(1)} %get-tuple-element.849, f32[4,512]{1,0:T(4,128)S(1)} %dynamic-slice_bitcast_fusion.7), kind=kLoop, calls=%fused_computation.66.clone.1 | loop fusion | flops 20971520 | bytes 41959424 | tf_op jit(solution)/shard_map/backward_attention/while/body/eval_jaxpr/convert_element_type | solution.py:240
  746.4 7.6 fusion.305
  754.0 7.5 fusion.307
  761.5 5.6 fusion.306
  793.5 86.0 %while.56 = (s32[]{:T(128)}, f32[1,2048,4,64]{1,3,2,0:T(8,128)}, f32[1,2048,4,64]{1,3,2,0:T(8,128)}, bf16[2,1,512,4,64]{2,4,3,1,0:T(8,128)(2,1)}, bf16[2,1,512,4...) while((s32[]{:T(128)}, f32[1,2048,4,64]{1,3,2,0:T(8,128)}, ...), condition=%wide.region_28.29_spmd.clone, body=%wide.region_26.28_spmd.clone.sunk | while | flops 2737436672 | bytes 273212096 | solution.py:263
  795.9 8.6 multiply_reduce_fusion.22
  806.8 10.4 %multiply_convert_fusion.13 = bf16[4,512,2048]{2,1,0:T(8,128)(2,1)} fusion(f32[4,512,2048]{2,1,0:T(8,128)} %get-tuple-element.837, f32[4,512,2048]{2,1,0:T(8,128)S(1)} %fusion.292, f32[4,512]{1,0:T(4,128)S(1)} %get-tuple-element.838, f32[4,512]{1,0:T(4,128)S(1)} %dynamic-slice_bitcast_fusion.6), kind=kLoop, calls=%fused_computation.32.clone.1 | loop fusion | flops 20971520 | bytes 41959424 | tf_op jit(solution)/shard_map/backward_attention/while/body/eval_jaxpr/convert_element_type | solution.py:240
  817.2 6.5 fusion.293
  823.7 7.5 fusion.295
  838.0 8.6 multiply_reduce_fusion.22
  848.9 10.4 %multiply_convert_fusion.13 = bf16[4,512,2048]{2,1,0:T(8,128)(2,1)} fusion(f32[4,512,2048]{2,1,0:T(8,128)} %get-tuple-element.837, f32[4,512,2048]{2,1,0:T(8,128)S(1)} %fusion.292, f32[4,512]{1,0:T(4,128)S(1)} %get-tuple-element.838, f32[4,512]{1,0:T(4,128)S(1)} %dynamic-slice_bitcast_fusion.6), kind=kLoop, calls=%fused_computation.32.clone.1 | loop fusion | flops 20971520 | bytes 41959424 | tf_op jit(solution)/shard_map/backward_attention/while/body/eval_jaxpr/convert_element_type | solution.py:240
  859.3 7.0 fusion.293
  866.3 7.5 fusion.295
  873.8 5.6 fusion.294
  908.1 5.1 all-to-all-start.6
  913.3 5.4 add_convert_fusion.2
  923.5 9.4 reduce-scatter.7.cloned.1.call-done
  934.5 40.2 %reduce-scatter.5.cloned.1.call-done = bf16[128,3,256]{2,0,1:T(8,128)(2,1)} async-done(((bf16[1024,3,256]{2,0,1:T(8,128)(2,1)}), bf16[128,3,256]{2,0,1:T(8,128)(2,1)}) %reduce-scatter.5.cloned.1.call-update) | async-done | bytes 196624 | tf_op jit(solution)/shard_map/weight_grads/reduce_scatter | solution.py:329
  1003.5 9.5 all-gather.2
  (452 shorter events, 307.8 us)
Async XLA Ops:
  7.2 20.2 %copy-start.71 = (bf16[128,256]{1,0:T(8,128)(2,1)S(1)}, bf16[128,256]{1,0:T(8,128)(2,1)}, u32[]{:S(2)}) copy-start(bf16[128,256]{1,0:T(8,128)(2,1)} %param.20) | copy-start | bytes 196612
  7.2 90.0 %all-gather.28.cloned.1.call-start = ((), (), s32[]{:S(2)}) async-start(), calls=%async_computation.25 | async-start | bytes 5242880 | tf_op jit(solution)/shard_map/group_inputs/all_gather | solution.py:73
  7.9 116.1 %all-gather.14.cloned.1.call-start = ((), (), s32[]{:S(2)}) async-start(), calls=%async_computation.14 | async-start | bytes 1769472 | tf_op jit(solution)/shard_map/weights/all_gather | solution.py:67
  9.7 302.4 %all-gather.30.cloned.1.call-start = ((), (), s32[]{:S(2)}) async-start(), calls=%async_computation.26 | async-start | bytes 5242880 | tf_op jit(solution)/shard_map/group_inputs/all_gather | solution.py:74
  23.3 16.9 %all-to-all-start = ((f32[8,2,4,6,256]{4,2,3,1,0:T(4,128)}), f32[8,2,4,6,256]{4,2,3,1,0:T(4,128)S(1)}, u32[]{:S(2)}, u32[]{:S(2)}) async-start(f32[8,2,4,6,256]{4,2,3,1,0:T(4,128)} %fusion.183), calls=%async_computation | async-start | bytes 786432 | tf_op jit(solution)/shard_map/modulation/all_to_all | solution.py:60
  26.8 291.0 %all-gather.20.cloned.1.call-start = ((), (), s32[]{:S(2)}) async-start(), calls=%async_computation.17 | async-start | bytes 2359296 | tf_op jit(solution)/shard_map/weights/all_gather | solution.py:67
  59.7 43.3 %copy-start.52 = (f32[2,4,6,1024]{3,2,1,0:T(8,128)}, f32[2,4,6,1024]{3,2,1,0:T(8,128)S(1)}, u32[]{:S(2)}) copy-start(f32[2,4,6,1024]{3,2,1,0:T(8,128)S(1)} %all_gather.40) | copy-start | bytes 589828
  128.5 8.0 collective-permute-start.3
  128.8 9.9 collective-permute-start.2
  134.8 36.8 %collective-permute-start.1 = (bf16[1,1024,256]{1,2,0:T(8,128)(2,1)}, bf16[1,1024,256]{1,2,0:T(8,128)(2,1)}, u32[]{:S(2)}, u32[]{:S(2)}) collective-permute-start(bf16[1,1024,256]{1,2,0:T(8,128)(2,1)} %get-tuple-element.602), channel_id=1, source_target_pairs={{0,4},{4,0},{1,5},{5,1},{2,6},{6,2},{3,7},{7,3},{8,12},{12,8},{9,1... | collective-permute-start | bytes 1572872 | tf_op jit(solution)/shard_map/forward/ppermute | solution.py:79
  135.1 37.9 %collective-permute-start = (bf16[1,1024,256]{1,2,0:T(8,128)(2,1)}, bf16[1,1024,256]{1,2,0:T(8,128)(2,1)}, u32[]{:S(2)}, u32[]{:S(2)}) collective-permute-start(bf16[1,1024,256]{1,2,0:T(8,128)(2,1)} %get-tuple-element.601), channel_id=1, source_target_pairs={{0,4},{4,0},{1,5},{5,1},{2,6},{6,2},{3,7},{7,3},{8,12},{12,8},{9,1... | collective-permute-start | bytes 1572872 | tf_op jit(solution)/shard_map/forward/ppermute | solution.py:79
  140.7 24.1 %copy-start.36 = (bf16[1024,256]{1,0:T(8,128)(2,1)S(1)}, bf16[1024,256]{1,0:T(8,128)(2,1)}, u32[]{:S(2)}) copy-start(bf16[1024,256]{1,0:T(8,128)(2,1)} %all_gather.43) | copy-start | bytes 1572868
  166.9 83.9 %all-to-all-start.3 = ((bf16[1,4,256,1024]{3,2,0,1:T(8,128)(2,1)}), bf16[1,4,256,1024]{3,2,0,1:T(8,128)(2,1)}, u32[]{:S(2)}, u32[]{:S(2)}) async-start(bf16[1,4,256,1024]{3,2,0,1:T(8,128)(2,1)} %bitcast.675), calls=%async_computation.3 | async-start | bytes 4194304 | tf_op jit(solution)/shard_map/forward/all_to_all | solution.py:105
  174.9 24.6 %copy-start.37 = (bf16[1024,256]{1,0:T(8,128)(2,1)S(1)}, bf16[1024,256]{1,0:T(8,128)(2,1)}, u32[]{:S(2)}) copy-start(bf16[1024,256]{1,0:T(8,128)(2,1)} %all_gather.43) | copy-start | bytes 1572868
  196.7 54.1 %copy-start.63 = (f32[2,1,4,512]{3,2,1,0:T(4,128)}, f32[2,1,4,512]{3,2,1,0:T(4,128)S(1)}, u32[]{:S(2)}) copy-start(f32[2,1,4,512]{3,2,1,0:T(4,128)S(1)} %get-tuple-element.898) | copy-start | bytes 49156
  196.7 54.1 %copy-start.6 = (bf16[1,2048,4,64]{1,3,2,0:T(8,128)(2,1)}, bf16[1,2048,4,64]{1,3,2,0:T(8,128)(2,1)S(1)}, u32[]{:S(2)}) copy-start(bf16[1,2048,4,64]{1,3,2,0:T(8,128)(2,1)S(1)} %get-tuple-element.971) | copy-start | bytes 3145732
  196.7 54.1 %copy-start.10 = (bf16[1,2048,4,64]{1,3,2,0:T(8,128)(2,1)}, bf16[1,2048,4,64]{1,3,2,0:T(8,128)(2,1)S(1)}, u32[]{:S(2)}) copy-start(bf16[1,2048,4,64]{1,3,2,0:T(8,128)(2,1)S(1)} %get-tuple-element.973) | copy-start | bytes 3145732
  250.8 53.2 %all-to-all-start.1 = ((bf16[1,4,256,1024]{3,2,0,1:T(8,128)(2,1)}), bf16[1,4,256,1024]{3,2,0,1:T(8,128)(2,1)}, u32[]{:S(2)}, u32[]{:S(2)}) async-start(bf16[1,4,256,1024]{3,2,0,1:T(8,128)(2,1)} %bitcast.676), calls=%async_computation.1 | async-start | bytes 4194304 | tf_op jit(solution)/shard_map/forward/all_to_all | solution.py:105
  255.4 70.6 %all-gather.18.cloned.1.call-start = ((), (), s32[]{:S(2)}) async-start(), calls=%async_computation.16 | async-start | bytes 2359296 | tf_op jit(solution)/shard_map/weights/all_gather | solution.py:67
  256.0 100.3 %all-gather.22.cloned.1.call-start = ((), (), s32[]{:S(2)}) async-start(), calls=%async_computation.18 | async-start | bytes 2621440 | tf_op jit(solution)/shard_map/forward/all_gather | solution.py:99
  257.6 48.6 %copy-start.16 = (f32[2,1,256,1024]{3,2,1,0:T(8,128)}, f32[2,1,256,1024]{3,2,1,0:T(8,128)S(1)}, u32[]{:S(2)}) copy-start(f32[2,1,256,1024]{3,2,1,0:T(8,128)S(1)} %convert_element_type.357) | copy-start | bytes 6291460
  257.8 52.1 %copy-start.72 = (f32[256]{0:T(256)}, f32[256]{0:T(256)S(1)}, u32[]{:S(2)}) copy-start(f32[256]{0:T(256)S(1)} %get-tuple-element.646) | copy-start | bytes 3076
  257.8 52.1 %copy-start.74 = (f32[256]{0:T(256)}, f32[256]{0:T(256)S(1)}, u32[]{:S(2)}) copy-start(f32[256]{0:T(256)S(1)} %get-tuple-element.647) | copy-start | bytes 3076
  311.2 126.3 %all-gather.16.cloned.1.call-start = ((), (), s32[]{:S(2)}) async-start(), calls=%async_computation.15 | async-start | bytes 2621440 | tf_op jit(solution)/shard_map/forward/all_gather | solution.py:99
  370.1 82.7 %all-to-all-start.7 = ((bf16[1,4,256,1024]{3,2,0,1:T(8,128)(2,1)}), bf16[1,4,256,1024]{3,2,0,1:T(8,128)(2,1)}, u32[]{:S(2)}, u32[]{:S(2)}) async-start(bf16[1,4,256,1024]{3,2,0,1:T(8,128)(2,1)} %bitcast.687), calls=%async_computation.7 | async-start | bytes 4194304 | tf_op jit(solution)/shard_map/backward_ffn/all_to_all | solution.py:105
  452.7 50.7 %all-to-all-start.5 = ((bf16[1,4,256,1024]{3,2,0,1:T(8,128)(2,1)}), bf16[1,4,256,1024]{3,2,0,1:T(8,128)(2,1)}, u32[]{:S(2)}, u32[]{:S(2)}) async-start(bf16[1,4,256,1024]{3,2,0,1:T(8,128)(2,1)} %bitcast.689), calls=%async_computation.5 | async-start | bytes 4194304 | tf_op jit(solution)/shard_map/backward_ffn/all_to_all | solution.py:105
  464.2 43.9 %copy-start.40 = (bf16[2,1,256,1024]{3,2,1,0:T(8,128)(2,1)S(1)}, bf16[2,1,256,1024]{3,2,1,0:T(8,128)(2,1)}, u32[]{:S(2)}) copy-start(bf16[2,1,256,1024]{3,2,1,0:T(8,128)(2,1)} %param.17) | copy-start | bytes 3145732
  503.4 52.4 %all-to-all-start.4 = ((bf16[1,4,256,1024]{3,2,0,1:T(8,128)(2,1)}), bf16[1,4,256,1024]{3,2,0,1:T(8,128)(2,1)}, u32[]{:S(2)}, u32[]{:S(2)}) async-start(bf16[1,4,256,1024]{3,2,0,1:T(8,128)(2,1)} %bitcast.688), calls=%async_computation.4 | async-start | bytes 4194304 | tf_op jit(solution)/shard_map/forward/all_to_all | solution.py:105
  555.8 85.9 %all-to-all-start.2 = ((bf16[1,4,256,1024]{3,2,0,1:T(8,128)(2,1)}), bf16[1,4,256,1024]{3,2,0,1:T(8,128)(2,1)}, u32[]{:S(2)}, u32[]{:S(2)}) async-start(bf16[1,4,256,1024]{3,2,0,1:T(8,128)(2,1)} %bitcast.686), calls=%async_computation.2 | async-start | bytes 4194304 | tf_op jit(solution)/shard_map/forward/all_to_all | solution.py:105
  560.3 110.8 %all-gather.26.cloned.1.call-start = ((), (), s32[]{:S(2)}) async-start(), calls=%async_computation.20 | async-start | bytes 2621440 | tf_op jit(solution)/shard_map/backward_attention/all_gather | solution.py:99
  567.9 208.6 %all-gather.24.cloned.1.call-start = ((), (), s32[]{:S(2)}) async-start(), calls=%async_computation.19 | async-start | bytes 2621440 | tf_op jit(solution)/shard_map/backward_attention/all_gather | solution.py:99
  649.2 269.6 %reduce-scatter.11.cloned.1.call-start = ((), (), s32[]{:S(2)}) async-start(), calls=%async_computation.24 | async-start | bytes 2359296 | tf_op jit(solution)/shard_map/weight_grads/reduce_scatter | solution.py:329
  662.8 257.9 %reduce-scatter.9.cloned.1.call-start = ((), (), s32[]{:S(2)}) async-start(), calls=%async_computation.23 | async-start | bytes 2359296 | tf_op jit(solution)/shard_map/weight_grads/reduce_scatter | solution.py:329
  771.0 8.9 collective-permute-start.6
  773.6 7.5 collective-permute-start.7
  787.9 120.2 %all-to-all-start.8 = ((bf16[1,4,256,1024]{3,2,0,1:T(8,128)(2,1)}), bf16[1,4,256,1024]{3,2,0,1:T(8,128)(2,1)}, u32[]{:S(2)}, u32[]{:S(2)}) async-start(bf16[1,4,256,1024]{3,2,0,1:T(8,128)(2,1)} %bitcast.685), calls=%async_computation.8 | async-start | bytes 4194304 | tf_op jit(solution)/shard_map/backward_attention/all_to_all | solution.py:105
  792.6 140.3 %reduce-scatter.7.cloned.1.call-start = ((), (), s32[]{:S(2)}) async-start(), calls=%async_computation.22 | async-start | bytes 589824 | tf_op jit(solution)/shard_map/weight_grads/reduce_scatter | solution.py:329
  882.4 14.8 %collective-permute-start.4 = (bf16[1,1024,256]{2,1,0:T(8,128)(2,1)}, bf16[1,1024,256]{2,1,0:T(8,128)(2,1)}, u32[]{:S(2)}, u32[]{:S(2)}) collective-permute-start(bf16[1,1024,256]{2,1,0:T(8,128)(2,1)} %copy.340), channel_id=1, source_target_pairs={{0,4},{4,0},{1,5},{5,1},{2,6},{6,2},{3,7},{7,3},{8,12},{12,8},{9,1... | collective-permute-start | bytes 1572872 | tf_op jit(solution)/shard_map/backward_attention/ppermute | solution.py:89
  886.0 12.4 %collective-permute-start.5 = (bf16[1,1024,256]{2,1,0:T(8,128)(2,1)}, bf16[1,1024,256]{2,1,0:T(8,128)(2,1)}, u32[]{:S(2)}, u32[]{:S(2)}) collective-permute-start(bf16[1,1024,256]{2,1,0:T(8,128)(2,1)} %copy.342), channel_id=1, source_target_pairs={{0,4},{4,0},{1,5},{5,1},{2,6},{6,2},{3,7},{7,3},{8,12},{12,8},{9,1... | collective-permute-start | bytes 1572872 | tf_op jit(solution)/shard_map/backward_attention/ppermute | solution.py:89
  908.1 71.3 %all-to-all-start.6 = ((bf16[1,4,256,1024]{3,2,0,1:T(8,128)(2,1)}), bf16[1,4,256,1024]{3,2,0,1:T(8,128)(2,1)}, u32[]{:S(2)}, u32[]{:S(2)}) async-start(bf16[1,4,256,1024]{3,2,0,1:T(8,128)(2,1)} %bitcast.93), calls=%async_computation.6 | async-start | bytes 4194304 | tf_op jit(solution)/shard_map/backward_attention/all_to_all | solution.py:105
  913.3 61.4 %reduce-scatter.5.cloned.1.call-start = ((), (), s32[]{:S(2)}) async-start(), calls=%async_computation.21 | async-start | bytes 1769472 | tf_op jit(solution)/shard_map/weight_grads/reduce_scatter | solution.py:329
  918.8 60.4 %copy-start.69 = (f32[1,1,1,1024]{3,1,2,0:T(1,128)S(1)}, f32[1,1,1,1024]{3,1,2,0:T(1,128)}, u32[]{:S(2)}) copy-start(f32[1,1,1,1024]{3,1,2,0:T(1,128)} %get-tuple-element.633) | copy-start | bytes 12292
  918.8 63.5 %copy-start.84 = (f32[256]{0:T(256)}, f32[256]{0:T(256)S(1)}, u32[]{:S(2)}) copy-start(f32[256]{0:T(256)S(1)} %add_rsqrt_fusion.2) | copy-start | bytes 3076
  918.8 63.5 %copy-start.85 = (f32[256]{0:T(256)}, f32[256]{0:T(256)S(1)}, u32[]{:S(2)}) copy-start(f32[256]{0:T(256)S(1)} %add_rsqrt_fusion.3) | copy-start | bytes 3076
  923.5 58.6 %copy-start.70 = (f32[1,1,1,1024]{3,1,2,0:T(1,128)S(1)}, f32[1,1,1,1024]{3,1,2,0:T(1,128)}, u32[]{:S(2)}) copy-start(f32[1,1,1,1024]{3,1,2,0:T(1,128)} %get-tuple-element.629) | copy-start | bytes 12292
  988.9 10.4 %all-to-all-start.9 = ((f32[4,1,3072]{2,1,0:T(1,128)}), f32[4,1,3072]{2,1,0:T(1,128)}, u32[]{:S(2)}, u32[]{:S(2)}) async-start(f32[4,1,3072]{2,1,0:T(1,128)} %reshape.1457), calls=%async_computation.13 | async-start | bytes 98304 | tf_op jit(solution)/shard_map/ada_grad/all_to_all | solution.py:318
  993.5 20.9 %copy-start.1 = (bf16[128,6,256]{2,0,1:T(8,128)(2,1)S(1)}, bf16[128,6,256]{2,0,1:T(8,128)(2,1)}, u32[]{:S(2)}) copy-start(bf16[128,6,256]{2,0,1:T(8,128)(2,1)} %param.23) | copy-start | bytes 1179652
  996.2 16.8 %copy-start.68 = (bf16[8,2,4,128]{3,0,2,1:T(8,128)(2,1)S(1)}, bf16[8,2,4,128]{3,0,2,1:T(8,128)(2,1)}, u32[]{:S(2)}) copy-start(bf16[8,2,4,128]{3,0,2,1:T(8,128)(2,1)} %copy-done.67) | copy-start | bytes 49156
  (85 other events, 505.3 us)
Sparse Core Ops, SparseCore 0:
  9.6 87.6 all-gather.27
  99.7 24.2 all-gather.13
  125.6 119.1 all-gather.29
  246.5 26.3 all-gather.19
  274.6 27.7 all-gather.17
  311.3 44.8 all-gather.21
  358.4 79.0 all-gather.15
  568.0 74.0 all-gather.25
  649.4 43.9 all-gather.23
  696.4 39.9 reduce-scatter.10
  739.7 41.1 reduce-scatter.8
  897.3 35.5 reduce-scatter.6
  936.2 38.3 reduce-scatter.4
where the time goes:
time: 1030 us; the launch traced here: 1020 us
  waiting for transfers between devices  430 us (42%)
  matrix products  264 us (26%)
  other arithmetic  141 us (14%)
  local copies, waits for them, and re-layouts  68 us (7%)
  blocking collectives  52.3 us (5%)
  starting transfers between devices  48.6 us (5%)
  between operations  15.9 us (2%)
    all_to_all x8, waiting for transfers between devices, scatter_tokens(): received = lax.all_to_all(parts, 'tensor', 1, 1, tiled=True)  237 us
    all_gather x4, waiting for transfers between devices, gather_tokens(): return lax.all_gather(values, 'tensor', axis=1, tiled=True)  86.3 us
    reduce_scatter x4, waiting for transfers between devices, on_device(): lax.psum_scatter(total.astype(jnp.bfloat16), ('dp', 'frame'), scatter_dim...  49.6 us
    convert_element_type x4, other arithmetic, attend_back(): grad_scores = (probs * (grad_probs - row_terms)).astype(jnp.bfloat16)  41.9 us
    all_to_all x8, starting transfers between devices, scatter_tokens(): received = lax.all_to_all(parts, 'tensor', 1, 1, tiled=True)  37.6 us
    all_gather x1, waiting for transfers between devices, on_device(): group_tokens = lax.all_gather(tokens[:, 0], 'tensor', axis=1, tiled=True)  36.2 us
    dot_general x4, matrix products, attend_back(): jnp.einsum('cqhe,ckhe->chqk', grad_block, value_heads, preferred_element_...  34.3 us
    dot_general x4, matrix products, attend_back(): jnp.einsum('chqk,ckhe->cqhe', grad_scores, key_heads, preferred_element_t...  30 us
  transfers between devices with their start and end apart: 31, of which 12 were waited for; matrix products, arithmetic and copies ran while one was open for 43% of the time, Pallas kernels for 0%

commit v1 on v0

--- a/solution.py
+++ b/solution.py
@@ -7,6 +7,18 @@
 HEAD_DIM = 64
 epsilon = 1e-06
 highest = lax.Precision.HIGHEST
+
+
+def doubled_up(x, axis, dim):
+    ways, here = (lax.axis_size(axis), lax.axis_index(axis))
+    grown, reach = (x, 1)
+    while reach < ways:
+        theirs = lax.ppermute(grown, axis, [(d, d ^ reach) for d in range(ways)])
+        mine_first = jnp.concatenate([grown, theirs], axis=dim)
+        theirs_first = jnp.concatenate([theirs, grown], axis=dim)
+        grown = jnp.where(here & reach == 0, mine_first, theirs_first)
+        reach = 2 * reach
+    return grown
 
 
 def normalize(values):
@@ -64,7 +76,7 @@
         modulation = lax.dynamic_index_in_dim(group_mod, group_index, axis=2, keepdims=False)
     with jax.named_scope("weights"):
         joint_weight, mixer_weight, upward_weight, downward_weight = (
-            lax.all_gather(w, ("dp", "frame"), axis=0, tiled=True)
+            doubled_up(w, ("dp", "frame"), 0)
             for w in (qkv_weight, out_weight, up_weight, down_weight)
         )
     residual = tokens[:, 0].astype(jnp.float32)

time: 1030 us -> 991 us (0.962)
  waiting for transfers between devices: 430 us -> 406 us
  local copies, waits for them, and re-layouts: 68 us -> 54.7 us
  blocking collectives: 52.3 us -> 39 us
  starting transfers between devices: 48.6 us -> 59.9 us
    all_gather x4, waiting for transfers between devices: 86.3 us -> 24.1 us  [gather_tokens(): return lax.all_gather(values, 'tensor', axis=1, tiled=True)]
    ppermute x0 -> x12, waiting for transfers between devices: none -> 43.3 us  [doubled_up(): theirs = lax.ppermute(grown, axis, [(d, d ^ reach) for d in range(ways)])]
    all_gather x3 -> x0, waiting for transfers between devices: 16.2 us -> none  [on_device(): lax.all_gather(w, ('dp', 'frame'), axis=0, tiled=True)]
    all_gather x1 -> x0, blocking collectives: 12.8 us -> none  [on_device(): lax.all_gather(w, ('dp', 'frame'), axis=0, tiled=True)]
    ppermute x0 -> x12, starting transfers between devices: none -> 11.7 us  [doubled_up(): theirs = lax.ppermute(grown, axis, [(d, d ^ reach) for d in range(ways)])]
    unnamed x204 -> x229, local copies, waits for them, and re-layouts: 28 us -> 25.1 us
  transfers between devices with their start and end apart: 31 -> 40, of which waited for: 12 -> 18; matrix products, arithmetic and copies ran while one was open for 43% -> 43% of each run, Pallas kernels for 0% -> 0%
where the time goes in v1:
time: 991 us; the launch traced here: 980 us
  waiting for transfers between devices  406 us (41%)
  matrix products  261 us (26%)
  other arithmetic  143 us (14%)
  starting transfers between devices  59.9 us (6%)
  local copies, waits for them, and re-layouts  54.7 us (6%)
  blocking collectives  39 us (4%)
  between operations  16.5 us (2%)
    all_to_all x8, waiting for transfers between devices, scatter_tokens(): received = lax.all_to_all(parts, 'tensor', 1, 1, tiled=True)  240 us
    reduce_scatter x4, waiting for transfers between devices, on_device(): lax.psum_scatter(total.astype(jnp.bfloat16), ('dp', 'frame'), scatter_dim...  50.9 us
    ppermute x12, waiting for transfers between devices, doubled_up(): theirs = lax.ppermute(grown, axis, [(d, d ^ reach) for d in range(ways)])  43.3 us
    convert_element_type x4, other arithmetic, attend_back(): grad_scores = (probs * (grad_probs - row_terms)).astype(jnp.bfloat16)  41.9 us
    all_gather x1, waiting for transfers between devices, on_device(): group_tokens = lax.all_gather(tokens[:, 0], 'tensor', axis=1, tiled=True)  41.1 us
    all_to_all x8, starting transfers between devices, scatter_tokens(): received = lax.all_to_all(parts, 'tensor', 1, 1, tiled=True)  37.3 us
    dot_general x4, matrix products, attend_back(): jnp.einsum('cqhe,ckhe->chqk', grad_block, value_heads, preferred_element_...  34.3 us
    dot_general x4, matrix products, attend_back(): jnp.einsum('chqk,ckhe->cqhe', grad_scores, key_heads, preferred_element_t...  30.1 us
  transfers between devices with their start and end apart: 40, of which 18 were waited for; matrix products, arithmetic and copies ran while one was open for 43% of the time, Pallas kernels for 0%

profile of v1, /device:TPU:0, one launch (start us, length us, event | category | flops | bytes accessed | tf_op | source)
XLA Modules:
  0.0 979.9 jit_solution(3880863354238048014)
XLA Ops:
  8.5 10.1 %all-gather.3 = s32[8,2,4]{2,1,0:T(2,128)S(1)} all-gather(s32[1,2,4]{2,1,0:T(2,128)} %bitcast.719), channel_id=1, replica_groups=mesh['dp'=4,'frame'=2,'tensor'=4] {'dp','frame'}, dimensions={0}, use_global_device_ids=true | all-gather | bytes 288 | tf_op jit(solution)/shard_map/modulation/all_gather | solution.py:62
  35.0 19.4 %all_gather.28 = f32[2,4,6,1024]{3,2,1,0:T(8,128)S(1)} all-gather(f32[2,4,6,256]{3,2,1,0:T(8,128)S(1)} %copy.329), channel_id=1, replica_groups=mesh['dp'=4,'frame'=2,'tensor'=4] {'tensor'}, dimensions={3}, use_global_device_ids=true | all-gather | bytes 245760 | tf_op jit(solution)/shard_map/modulation/all_gather | solution.py:73
  56.1 41.1 %all-gather.19.cloned.1.call-done = bf16[2,1,1024,1024]{3,2,1,0:T(8,128)(2,1)} async-done(((bf16[2,1,256,1024]{3,2,1,0:T(8,128)(2,1)}), bf16[2,1,1024,1024]{3,2,1,0:T(8,128)(2,1)}) %all-gather.19.cloned.1.call-update) | async-done | bytes 4194320 | tf_op jit(solution)/shard_map/group_inputs/all_gather | solution.py:85
  124.6 20.7 %while.55 = (s32[]{:T(128)}, bf16[2,1,512,4,64]{2,4,3,1,0:T(8,128)(2,1)S(1)}, f32[2,1,4,512]{3,2,1,0:T(4,128)S(1)}, bf16[2,1,512,4,64]{2,4,3,1,0:T(8,128)(2,1)S(...) while((s32[]{:T(128)}, ...), condition=%wide.region_16.17_spmd, body=%wide.region_13.16_spmd.sunk | while | flops 1111619584 | bytes 53018712 | solution.py:164
  157.6 20.6 %while.54 = (s32[]{:T(128)}, bf16[2,1,512,4,64]{2,4,3,1,0:T(8,128)(2,1)S(1)}, f32[2,1,4,512]{3,2,1,0:T(4,128)S(1)}, bf16[2,1,512,4,64]{2,4,3,1,0:T(8,128)(2,1)S(...) while((s32[]{:T(128)}, ...), condition=%wide.region_6.7_spmd, body=%wide.region_3.6_spmd.sunk | while | flops 1111619584 | bytes 53018712 | solution.py:164
  183.1 39.6 %all-to-all-done.3 = bf16[1,4,256,1024]{3,2,0,1:T(8,128)(2,1)} async-done(((bf16[1,4,256,1024]{3,2,0,1:T(8,128)(2,1)}), bf16[1,4,256,1024]{3,2,0,1:T(8,128)(2,1)}, u32[]{:S(2)}, u32[]{:S(2)}) %all-to-all-start.3) | async-done | bytes 2097184 | tf_op jit(solution)/shard_map/forward/all_to_all | solution.py:117
  232.0 43.7 %all-to-all-done.1 = bf16[1,4,256,1024]{3,2,0,1:T(8,128)(2,1)} async-done(((bf16[1,4,256,1024]{3,2,0,1:T(8,128)(2,1)}), bf16[1,4,256,1024]{3,2,0,1:T(8,128)(2,1)}, u32[]{:S(2)}, u32[]{:S(2)}) %all-to-all-start.1) | async-done | bytes 2097184 | tf_op jit(solution)/shard_map/forward/all_to_all | solution.py:117
  286.1 11.9 %collective-permute-done.9 = bf16[256,1024]{1,0:T(8,128)(2,1)S(1)} collective-permute-done((bf16[256,1024]{1,0:T(8,128)(2,1)S(1)}, bf16[256,1024]{1,0:T(8,128)(2,1)S(1)}, u32[]{:S(2)}, u32[]{:S(2)}) %collective-permute-start.9) | collective-permute-done | bytes 524320 | tf_op jit(solution)/shard_map/weights/ppermute | solution.py:16
  301.0 7.4 collective-permute-done.12
  310.5 5.6 fusion.107
  317.4 8.5 collective-permute-done.10
  326.2 5.3 fusion.140
  331.5 14.4 %collective-permute-done.13 = bf16[512,1024]{1,0:T(8,128)(2,1)} collective-permute-done((bf16[512,1024]{1,0:T(8,128)(2,1)S(1)}, bf16[512,1024]{1,0:T(8,128)(2,1)}, u32[]{:S(2)}, u32[]{:S(2)}) %collective-permute-start.13) | collective-permute-done | bytes 1048608 | tf_op jit(solution)/shard_map/weights/ppermute | solution.py:16
  345.9 6.0 fusion.125
  352.0 6.6 convolution_convert_fusion
  363.5 23.8 %all-gather.11.cloned.1.call-done = bf16[1,1024,1024]{2,1,0:T(8,128)(2,1)} async-done(((bf16[1,256,1024]{2,1,0:T(8,128)(2,1)}), bf16[1,1024,1024]{2,1,0:T(8,128)(2,1)}) %all-gather.11.cloned.1.call-update) | async-done | bytes 2097168 | tf_op jit(solution)/shard_map/forward/all_gather | solution.py:111
  387.3 5.3 fusion.144
  392.6 6.8 fusion.118
  400.7 6.0 convolution_convert_fusion.1
  406.7 10.6 %all-to-all-done.7 = bf16[1,4,256,1024]{3,2,0,1:T(8,128)(2,1)} async-done(((bf16[1,4,256,1024]{3,2,0,1:T(8,128)(2,1)}), bf16[1,4,256,1024]{3,2,0,1:T(8,128)(2,1)}, u32[]{:S(2)}, u32[]{:S(2)}) %all-to-all-start.7) | async-done | bytes 2097184 | tf_op jit(solution)/shard_map/backward_ffn/all_to_all | solution.py:117
  421.8 7.7 convolution_convert_fusion.2
  429.5 40.7 %all-to-all-done.5 = bf16[1,4,256,1024]{3,2,0,1:T(8,128)(2,1)} async-done(((bf16[1,4,256,1024]{3,2,0,1:T(8,128)(2,1)}), bf16[1,4,256,1024]{3,2,0,1:T(8,128)(2,1)}, u32[]{:S(2)}, u32[]{:S(2)}) %all-to-all-start.5) | async-done | bytes 2097184 | tf_op jit(solution)/shard_map/backward_ffn/all_to_all | solution.py:117
  476.3 8.3 convolution_convert_fusion.4
  484.6 38.0 %all-to-all-done.4 = bf16[1,4,256,1024]{3,2,0,1:T(8,128)(2,1)} async-done(((bf16[1,4,256,1024]{3,2,0,1:T(8,128)(2,1)}), bf16[1,4,256,1024]{3,2,0,1:T(8,128)(2,1)}, u32[]{:S(2)}, u32[]{:S(2)}) %all-to-all-start.4) | async-done | bytes 2097184 | tf_op jit(solution)/shard_map/forward/all_to_all | solution.py:117
  541.2 67.0 %all-to-all-done.2 = bf16[1,4,256,1024]{3,2,0,1:T(8,128)(2,1)} async-done(((bf16[1,4,256,1024]{3,2,0,1:T(8,128)(2,1)}), bf16[1,4,256,1024]{3,2,0,1:T(8,128)(2,1)}, u32[]{:S(2)}, u32[]{:S(2)}) %all-to-all-start.2) | async-done | bytes 2097184 | tf_op jit(solution)/shard_map/forward/all_to_all | solution.py:117
  644.7 87.0 %while.57 = (s32[]{:T(128)}, f32[1,2048,4,64]{1,3,2,0:T(8,128)}, f32[1,2048,4,64]{1,3,2,0:T(8,128)}, bf16[2,1,512,4,64]{2,4,3,1,0:T(8,128)(2,1)}, bf16[2,1,512,4...) while((s32[]{:T(128)}, f32[1,2048,4,64]{1,3,2,0:T(8,128)}, ...), condition=%wide.region_39.40_spmd.clone, body=%wide.region_37.39_spmd.clone.sunk | while | flops 2737436672 | bytes 273212096 | solution.py:275
  647.1 8.6 multiply_reduce_fusion.23
  658.0 10.5 %multiply_convert_fusion.14 = bf16[4,512,2048]{2,1,0:T(8,128)(2,1)} fusion(f32[4,512,2048]{2,1,0:T(8,128)} %get-tuple-element.844, f32[4,512,2048]{2,1,0:T(8,128)S(1)} %fusion.288, f32[4,512]{1,0:T(4,128)S(1)} %get-tuple-element.845, f32[4,512]{1,0:T(4,128)S(1)} %dynamic-slice_bitcast_fusion.7), kind=kLoop, calls=%fused_computation.66.clone.1 | loop fusion | flops 20971520 | bytes 41959424 | tf_op jit(solution)/shard_map/backward_attention/while/body/eval_jaxpr/convert_element_type | solution.py:252
  668.4 6.9 fusion.289
  675.3 7.5 fusion.291
  689.6 8.6 multiply_reduce_fusion.23
  700.5 10.5 %multiply_convert_fusion.14 = bf16[4,512,2048]{2,1,0:T(8,128)(2,1)} fusion(f32[4,512,2048]{2,1,0:T(8,128)} %get-tuple-element.844, f32[4,512,2048]{2,1,0:T(8,128)S(1)} %fusion.288, f32[4,512]{1,0:T(4,128)S(1)} %get-tuple-element.845, f32[4,512]{1,0:T(4,128)S(1)} %dynamic-slice_bitcast_fusion.7), kind=kLoop, calls=%fused_computation.66.clone.1 | loop fusion | flops 20971520 | bytes 41959424 | tf_op jit(solution)/shard_map/backward_attention/while/body/eval_jaxpr/convert_element_type | solution.py:252
  711.0 7.5 fusion.289
  718.5 7.6 fusion.291
  726.0 5.6 fusion.290
  755.9 86.0 %while.56 = (s32[]{:T(128)}, f32[1,2048,4,64]{1,3,2,0:T(8,128)}, f32[1,2048,4,64]{1,3,2,0:T(8,128)}, bf16[2,1,512,4,64]{2,4,3,1,0:T(8,128)(2,1)}, bf16[2,1,512,4...) while((s32[]{:T(128)}, f32[1,2048,4,64]{1,3,2,0:T(8,128)}, ...), condition=%wide.region_28.29_spmd.clone, body=%wide.region_26.28_spmd.clone.sunk | while | flops 2737436672 | bytes 273212096 | solution.py:275
  758.4 8.6 multiply_reduce_fusion.22
  769.3 10.5 %multiply_convert_fusion.13 = bf16[4,512,2048]{2,1,0:T(8,128)(2,1)} fusion(f32[4,512,2048]{2,1,0:T(8,128)} %get-tuple-element.833, f32[4,512,2048]{2,1,0:T(8,128)S(1)} %fusion.276, f32[4,512]{1,0:T(4,128)S(1)} %get-tuple-element.834, f32[4,512]{1,0:T(4,128)S(1)} %dynamic-slice_bitcast_fusion.6), kind=kLoop, calls=%fused_computation.32.clone.1 | loop fusion | flops 20971520 | bytes 41959424 | tf_op jit(solution)/shard_map/backward_attention/while/body/eval_jaxpr/convert_element_type | solution.py:252
  779.7 6.5 fusion.277
  786.2 7.5 fusion.279
  800.5 8.6 multiply_reduce_fusion.22
  811.4 10.5 %multiply_convert_fusion.13 = bf16[4,512,2048]{2,1,0:T(8,128)(2,1)} fusion(f32[4,512,2048]{2,1,0:T(8,128)} %get-tuple-element.833, f32[4,512,2048]{2,1,0:T(8,128)S(1)} %fusion.276, f32[4,512]{1,0:T(4,128)S(1)} %get-tuple-element.834, f32[4,512]{1,0:T(4,128)S(1)} %dynamic-slice_bitcast_fusion.6), kind=kLoop, calls=%fused_computation.32.clone.1 | loop fusion | flops 20971520 | bytes 41959424 | tf_op jit(solution)/shard_map/backward_attention/while/body/eval_jaxpr/convert_element_type | solution.py:252
  821.8 7.0 fusion.277
  828.9 7.5 fusion.279
  836.4 5.6 fusion.278
  880.5 10.9 %reduce-scatter.7.cloned.1.call-done = bf16[128,256]{1,0:T(8,128)(2,1)} async-done(((bf16[1024,256]{1,0:T(8,128)(2,1)}), bf16[128,256]{1,0:T(8,128)(2,1)}) %reduce-scatter.7.cloned.1.call-update) | async-done | bytes 65552 | tf_op jit(solution)/shard_map/weight_grads/reduce_scatter | solution.py:341
  892.8 40.0 %reduce-scatter.5.cloned.1.call-done = bf16[128,3,256]{2,0,1:T(8,128)(2,1)} async-done(((bf16[1024,3,256]{2,0,1:T(8,128)(2,1)}), bf16[128,3,256]{2,0,1:T(8,128)(2,1)}) %reduce-scatter.5.cloned.1.call-update) | async-done | bytes 196624 | tf_op jit(solution)/shard_map/weight_grads/reduce_scatter | solution.py:341
  961.6 9.5 all-gather.2
  (499 shorter events, 323.7 us)
Async XLA Ops:
  7.2 90.0 %all-gather.19.cloned.1.call-start = ((), (), s32[]{:S(2)}) async-start(), calls=%async_computation.22 | async-start | bytes 5242880 | tf_op jit(solution)/shard_map/group_inputs/all_gather | solution.py:85
  7.9 11.4 %collective-permute-start.5 = (bf16[128,256]{1,0:T(8,128)(2,1)}, bf16[128,256]{1,0:T(8,128)(2,1)S(1)}, u32[]{:S(2)}, u32[]{:S(2)}) collective-permute-start(bf16[128,256]{1,0:T(8,128)(2,1)} %param.20), channel_id=1, source_target_pairs={{0,4},{4,0},{8,12},{12,8},{16,20},{20,16},{24,28},{28,24},{1,5},{5... | collective-permute-start | bytes 196616 | tf_op jit(solution)/shard_map/weights/ppermute | solution.py:16
  20.2 6.6 collective-permute-start.6
  22.6 12.3 %all-to-all-start = ((f32[8,2,4,6,256]{4,2,3,1,0:T(4,128)}), f32[8,2,4,6,256]{4,2,3,1,0:T(4,128)S(1)}, u32[]{:S(2)}, u32[]{:S(2)}) async-start(f32[8,2,4,6,256]{4,2,3,1,0:T(4,128)} %fusion.183), calls=%async_computation | async-start | bytes 786432 | tf_op jit(solution)/shard_map/modulation/all_to_all | solution.py:72
  26.1 284.4 %all-gather.21.cloned.1.call-start = ((), (), s32[]{:S(2)}) async-start(), calls=%async_computation.23 | async-start | bytes 5242880 | tf_op jit(solution)/shard_map/group_inputs/all_gather | solution.py:86
  26.1 3.5 collective-permute-start
  27.7 118.4 %collective-permute-start.7 = (bf16[512,256]{1,0:T(8,128)(2,1)}, bf16[512,256]{1,0:T(8,128)(2,1)}, u32[]{:S(2)}, u32[]{:S(2)}) collective-permute-start(bf16[512,256]{1,0:T(8,128)(2,1)} %maximum_select_fusion.10), channel_id=1, source_target_pairs={{0,16},{4,20},{8,24},{12,28},{16,0},{20,4},{24,8},{28,12},{1,17},{... | collective-permute-start | bytes 786440 | tf_op jit(solution)/shard_map/weights/ppermute | solution.py:16
  29.8 26.0 %collective-permute-start.1 = (bf16[256,3,256]{2,0,1:T(8,128)(2,1)S(1)}, bf16[256,3,256]{2,0,1:T(8,128)(2,1)S(1)}, u32[]{:S(2)}, u32[]{:S(2)}) collective-permute-start(bf16[256,3,256]{2,0,1:T(8,128)(2,1)S(1)} %maximum_select_fusion.9), channel_id=1, source_target_pairs={{0,8},{4,12},{8,0},{12,4},{16,24},{20,28},{24,16},{28,20},{1,9},{5... | collective-permute-start | bytes 1179656 | tf_op jit(solution)/shard_map/weights/ppermute | solution.py:16
  56.0 51.2 %collective-permute-start.2 = (bf16[512,3,256]{2,0,1:T(8,128)(2,1)S(1)}, bf16[512,3,256]{2,0,1:T(8,128)(2,1)S(1)}, u32[]{:S(2)}, u32[]{:S(2)}) collective-permute-start(bf16[512,3,256]{2,0,1:T(8,128)(2,1)S(1)} %maximum_select_fusion.5), channel_id=1, source_target_pairs={{0,16},{4,20},{8,24},{12,28},{16,0},{20,4},{24,8},{28,12},{1,17},{... | collective-permute-start | bytes 2359304 | tf_op jit(solution)/shard_map/weights/ppermute | solution.py:16
  112.9 8.5 collective-permute-start.15
  112.9 10.6 %collective-permute-start.14 = (bf16[1,1024,256]{1,2,0:T(8,128)(2,1)}, bf16[1,1024,256]{1,2,0:T(8,128)(2,1)}, u32[]{:S(2)}, u32[]{:S(2)}) collective-permute-start(bf16[1,1024,256]{1,2,0:T(8,128)(2,1)} %get-tuple-element.606), channel_id=1, source_target_pairs={{0,4},{4,0},{1,5},{5,1},{2,6},{6,2},{3,7},{7,3},{8,12},{12,8},{9,1... | collective-permute-start | bytes 1572872 | tf_op jit(solution)/shard_map/forward/ppermute | solution.py:91
  119.6 35.5 %collective-permute-start.4 = (bf16[1,1024,256]{1,2,0:T(8,128)(2,1)}, bf16[1,1024,256]{1,2,0:T(8,128)(2,1)}, u32[]{:S(2)}, u32[]{:S(2)}) collective-permute-start(bf16[1,1024,256]{1,2,0:T(8,128)(2,1)} %get-tuple-element.602), channel_id=1, source_target_pairs={{0,4},{4,0},{1,5},{5,1},{2,6},{6,2},{3,7},{7,3},{8,12},{12,8},{9,1... | collective-permute-start | bytes 1572872 | tf_op jit(solution)/shard_map/forward/ppermute | solution.py:91
  119.6 36.8 %collective-permute-start.3 = (bf16[1,1024,256]{1,2,0:T(8,128)(2,1)}, bf16[1,1024,256]{1,2,0:T(8,128)(2,1)}, u32[]{:S(2)}, u32[]{:S(2)}) collective-permute-start(bf16[1,1024,256]{1,2,0:T(8,128)(2,1)} %get-tuple-element.601), channel_id=1, source_target_pairs={{0,4},{4,0},{1,5},{5,1},{2,6},{6,2},{3,7},{7,3},{8,12},{12,8},{9,1... | collective-permute-start | bytes 1572872 | tf_op jit(solution)/shard_map/forward/ppermute | solution.py:91
  150.4 72.2 %all-to-all-start.3 = ((bf16[1,4,256,1024]{3,2,0,1:T(8,128)(2,1)}), bf16[1,4,256,1024]{3,2,0,1:T(8,128)(2,1)}, u32[]{:S(2)}, u32[]{:S(2)}) async-start(bf16[1,4,256,1024]{3,2,0,1:T(8,128)(2,1)} %bitcast.664), calls=%async_computation.3 | async-start | bytes 4194304 | tf_op jit(solution)/shard_map/forward/all_to_all | solution.py:117
  179.7 47.7 %copy-start.35 = (bf16[2,1,256,1024]{3,2,1,0:T(8,128)(2,1)S(1)}, bf16[2,1,256,1024]{3,2,1,0:T(8,128)(2,1)}, u32[]{:S(2)}) copy-start(bf16[2,1,256,1024]{3,2,1,0:T(8,128)(2,1)} %param.16) | copy-start | bytes 3145732
  222.7 53.0 %all-to-all-start.1 = ((bf16[1,4,256,1024]{3,2,0,1:T(8,128)(2,1)}), bf16[1,4,256,1024]{3,2,0,1:T(8,128)(2,1)}, u32[]{:S(2)}, u32[]{:S(2)}) async-start(bf16[1,4,256,1024]{3,2,0,1:T(8,128)(2,1)} %bitcast.666), calls=%async_computation.1 | async-start | bytes 4194304 | tf_op jit(solution)/shard_map/forward/all_to_all | solution.py:117
  227.1 99.1 %all-gather.13.cloned.1.call-start = ((), (), s32[]{:S(2)}) async-start(), calls=%async_computation.15 | async-start | bytes 2621440 | tf_op jit(solution)/shard_map/forward/all_gather | solution.py:111
  227.6 50.2 %copy-start.16 = (f32[2,1,256,1024]{3,2,1,0:T(8,128)}, f32[2,1,256,1024]{3,2,1,0:T(8,128)S(1)}, u32[]{:S(2)}) copy-start(f32[2,1,256,1024]{3,2,1,0:T(8,128)S(1)} %convert_element_type.357) | copy-start | bytes 6291460
  228.1 49.8 %copy-start.83 = (f32[256]{0:T(256)}, f32[256]{0:T(256)S(1)}, u32[]{:S(2)}) copy-start(f32[256]{0:T(256)S(1)} %get-tuple-element.640) | copy-start | bytes 3076
  228.1 49.8 %copy-start.85 = (f32[256]{0:T(256)}, f32[256]{0:T(256)S(1)}, u32[]{:S(2)}) copy-start(f32[256]{0:T(256)S(1)} %get-tuple-element.641) | copy-start | bytes 3076
  281.3 106.0 %all-gather.11.cloned.1.call-start = ((), (), s32[]{:S(2)}) async-start(), calls=%async_computation.14 | async-start | bytes 2621440 | tf_op jit(solution)/shard_map/forward/all_gather | solution.py:111
  281.4 1.6 collective-permute-start.8
  281.5 3.2 collective-permute-start.11
  283.1 14.9 %collective-permute-start.9 = (bf16[256,1024]{1,0:T(8,128)(2,1)S(1)}, bf16[256,1024]{1,0:T(8,128)(2,1)S(1)}, u32[]{:S(2)}, u32[]{:S(2)}) collective-permute-start(bf16[256,1024]{1,0:T(8,128)(2,1)S(1)} %maximum_select_fusion.7), channel_id=1, source_target_pairs={{0,8},{4,12},{8,0},{12,4},{16,24},{20,28},{24,16},{28,20},{1,9},{5... | collective-permute-start | bytes 1572872 | tf_op jit(solution)/shard_map/weights/ppermute | solution.py:16
  284.8 23.6 %collective-permute-start.12 = (bf16[256,1024]{1,0:T(8,128)(2,1)S(1)}, bf16[256,1024]{1,0:T(8,128)(2,1)S(1)}, u32[]{:S(2)}, u32[]{:S(2)}) collective-permute-start(bf16[256,1024]{1,0:T(8,128)(2,1)S(1)} %maximum_select_fusion.8), channel_id=1, source_target_pairs={{0,8},{4,12},{8,0},{12,4},{16,24},{20,28},{24,16},{28,20},{1,9},{5... | collective-permute-start | bytes 1572872 | tf_op jit(solution)/shard_map/weights/ppermute | solution.py:16
  299.5 26.3 %collective-permute-start.10 = (bf16[512,1024]{1,0:T(8,128)(2,1)}, bf16[512,1024]{1,0:T(8,128)(2,1)}, u32[]{:S(2)}, u32[]{:S(2)}) collective-permute-start(bf16[512,1024]{1,0:T(8,128)(2,1)} %maximum_select_fusion.3), channel_id=1, source_target_pairs={{0,16},{4,20},{8,24},{12,28},{16,0},{20,4},{24,8},{28,12},{1,17},{... | collective-permute-start | bytes 3145736 | tf_op jit(solution)/shard_map/weights/ppermute | solution.py:16
  308.9 112.9 %copy-start.52 = (bf16[512,1024]{1,0:T(8,128)(2,1)}, bf16[512,1024]{1,0:T(8,128)(2,1)S(1)}, u32[]{:S(2)}) copy-start(bf16[512,1024]{1,0:T(8,128)(2,1)S(1)} %maximum_select_fusion.4) | copy-start | bytes 3145732
  308.9 37.0 %collective-permute-start.13 = (bf16[512,1024]{1,0:T(8,128)(2,1)S(1)}, bf16[512,1024]{1,0:T(8,128)(2,1)}, u32[]{:S(2)}, u32[]{:S(2)}) collective-permute-start(bf16[512,1024]{1,0:T(8,128)(2,1)S(1)} %maximum_select_fusion.4), channel_id=1, source_target_pairs={{0,16},{4,20},{8,24},{12,28},{16,0},{20,4},{24,8},{28,12},{1,17},{... | collective-permute-start | bytes 3145736 | tf_op jit(solution)/shard_map/weights/ppermute | solution.py:16
  358.6 58.8 %all-to-all-start.7 = ((bf16[1,4,256,1024]{3,2,0,1:T(8,128)(2,1)}), bf16[1,4,256,1024]{3,2,0,1:T(8,128)(2,1)}, u32[]{:S(2)}, u32[]{:S(2)}) async-start(bf16[1,4,256,1024]{3,2,0,1:T(8,128)(2,1)} %bitcast.667), calls=%async_computation.7 | async-start | bytes 4194304 | tf_op jit(solution)/shard_map/backward_ffn/all_to_all | solution.py:117
  417.4 52.9 %all-to-all-start.5 = ((bf16[1,4,256,1024]{3,2,0,1:T(8,128)(2,1)}), bf16[1,4,256,1024]{3,2,0,1:T(8,128)(2,1)}, u32[]{:S(2)}, u32[]{:S(2)}) async-start(bf16[1,4,256,1024]{3,2,0,1:T(8,128)(2,1)} %bitcast.669), calls=%async_computation.5 | async-start | bytes 4194304 | tf_op jit(solution)/shard_map/backward_ffn/all_to_all | solution.py:117
  470.3 52.3 %all-to-all-start.4 = ((bf16[1,4,256,1024]{3,2,0,1:T(8,128)(2,1)}), bf16[1,4,256,1024]{3,2,0,1:T(8,128)(2,1)}, u32[]{:S(2)}, u32[]{:S(2)}) async-start(bf16[1,4,256,1024]{3,2,0,1:T(8,128)(2,1)} %bitcast.668), calls=%async_computation.4 | async-start | bytes 4194304 | tf_op jit(solution)/shard_map/forward/all_to_all | solution.py:117
  522.5 85.7 %all-to-all-start.2 = ((bf16[1,4,256,1024]{3,2,0,1:T(8,128)(2,1)}), bf16[1,4,256,1024]{3,2,0,1:T(8,128)(2,1)}, u32[]{:S(2)}, u32[]{:S(2)}) async-start(bf16[1,4,256,1024]{3,2,0,1:T(8,128)(2,1)} %bitcast.665), calls=%async_computation.2 | async-start | bytes 4194304 | tf_op jit(solution)/shard_map/forward/all_to_all | solution.py:117
  527.0 110.8 %all-gather.17.cloned.1.call-start = ((), (), s32[]{:S(2)}) async-start(), calls=%async_computation.17 | async-start | bytes 2621440 | tf_op jit(solution)/shard_map/backward_attention/all_gather | solution.py:111
  534.7 203.8 %all-gather.15.cloned.1.call-start = ((), (), s32[]{:S(2)}) async-start(), calls=%async_computation.16 | async-start | bytes 2621440 | tf_op jit(solution)/shard_map/backward_attention/all_gather | solution.py:111
  615.7 260.0 %reduce-scatter.11.cloned.1.call-start = ((), (), s32[]{:S(2)}) async-start(), calls=%async_computation.21 | async-start | bytes 2359296 | tf_op jit(solution)/shard_map/weight_grads/reduce_scatter | solution.py:341
  629.5 248.1 %reduce-scatter.9.cloned.1.call-start = ((), (), s32[]{:S(2)}) async-start(), calls=%async_computation.20 | async-start | bytes 2359296 | tf_op jit(solution)/shard_map/weight_grads/reduce_scatter | solution.py:341
  734.7 7.6 collective-permute-start.18
  736.1 7.4 collective-permute-start.19
  750.3 114.9 %all-to-all-start.8 = ((bf16[1,4,256,1024]{3,2,0,1:T(8,128)(2,1)}), bf16[1,4,256,1024]{3,2,0,1:T(8,128)(2,1)}, u32[]{:S(2)}, u32[]{:S(2)}) async-start(bf16[1,4,256,1024]{3,2,0,1:T(8,128)(2,1)} %bitcast.663), calls=%async_computation.8 | async-start | bytes 4194304 | tf_op jit(solution)/shard_map/backward_attention/all_to_all | solution.py:117
  755.0 136.3 %reduce-scatter.7.cloned.1.call-start = ((), (), s32[]{:S(2)}) async-start(), calls=%async_computation.19 | async-start | bytes 589824 | tf_op jit(solution)/shard_map/weight_grads/reduce_scatter | solution.py:341
  845.0 10.7 %collective-permute-start.16 = (bf16[1,1024,256]{2,1,0:T(8,128)(2,1)}, bf16[1,1024,256]{2,1,0:T(8,128)(2,1)}, u32[]{:S(2)}, u32[]{:S(2)}) collective-permute-start(bf16[1,1024,256]{2,1,0:T(8,128)(2,1)} %copy.332), channel_id=1, source_target_pairs={{0,4},{4,0},{1,5},{5,1},{2,6},{6,2},{3,7},{7,3},{8,12},{12,8},{9,1... | collective-permute-start | bytes 1572872 | tf_op jit(solution)/shard_map/backward_attention/ppermute | solution.py:101
  847.2 9.8 collective-permute-start.17
  865.2 72.2 %all-to-all-start.6 = ((bf16[1,4,256,1024]{3,2,0,1:T(8,128)(2,1)}), bf16[1,4,256,1024]{3,2,0,1:T(8,128)(2,1)}, u32[]{:S(2)}, u32[]{:S(2)}) async-start(bf16[1,4,256,1024]{3,2,0,1:T(8,128)(2,1)} %bitcast.93), calls=%async_computation.6 | async-start | bytes 4194304 | tf_op jit(solution)/shard_map/backward_attention/all_to_all | solution.py:117
  870.5 62.3 %reduce-scatter.5.cloned.1.call-start = ((), (), s32[]{:S(2)}) async-start(), calls=%async_computation.18 | async-start | bytes 1769472 | tf_op jit(solution)/shard_map/weight_grads/reduce_scatter | solution.py:341
  875.7 64.8 %copy-start.95 = (f32[256]{0:T(256)}, f32[256]{0:T(256)S(1)}, u32[]{:S(2)}) copy-start(f32[256]{0:T(256)S(1)} %add_rsqrt_fusion.2) | copy-start | bytes 3076
  875.7 64.8 %copy-start.96 = (f32[256]{0:T(256)}, f32[256]{0:T(256)S(1)}, u32[]{:S(2)}) copy-start(f32[256]{0:T(256)S(1)} %add_rsqrt_fusion.3) | copy-start | bytes 3076
  879.4 57.8 %copy-start.81 = (f32[1,1,1,1024]{3,1,2,0:T(1,128)S(1)}, f32[1,1,1,1024]{3,1,2,0:T(1,128)}, u32[]{:S(2)}) copy-start(f32[1,1,1,1024]{3,1,2,0:T(1,128)} %get-tuple-element.633) | copy-start | bytes 12292
  947.1 10.4 %all-to-all-start.9 = ((f32[4,1,3072]{2,1,0:T(1,128)}), f32[4,1,3072]{2,1,0:T(1,128)}, u32[]{:S(2)}, u32[]{:S(2)}) async-start(f32[4,1,3072]{2,1,0:T(1,128)} %reshape.1457), calls=%async_computation.13 | async-start | bytes 98304 | tf_op jit(solution)/shard_map/ada_grad/all_to_all | solution.py:330
  (107 other events, 855.2 us)
Sparse Core Ops, SparseCore 0:
  9.6 87.5 all-gather.18
  98.7 100.7 all-gather.20
  281.4 44.6 all-gather.12
  328.2 59.0 all-gather.10
  534.8 73.8 all-gather.16
  615.9 43.7 all-gather.14
  663.0 39.9 reduce-scatter.10
  706.2 41.1 reduce-scatter.8
  855.7 35.5 reduce-scatter.6
  894.5 38.3 reduce-scatter.4
